TPU v7x, 32 devices: a whole 2x2x4 slice. The times are simulated.
32 devices in a mesh: tm: 8 (over z, y), mp: 4 (over x, core).
Axes of the slice: x: 2, y: 2, z: 4, core: 2. Of those that a mesh axis runs over, the one named last changes fastest.
Arguments:
- latents: float32 [4, 8, 4, 4096], P(None, 'tm'), may hold values from -6 to 6
- noise: float32 [4, 8, 4, 4096], P(None, 'tm'), may hold values from -6 to 6
- start_step: int32 [4], replicated, may hold values from 8 to 999
- slide: int32 [4], replicated, may hold values from 1 to 8, as said below
- w_in: float32 [4, 320], replicated, may hold values from -3 to 3
- w_gate: bfloat16 [320, 1280], P(None, 'mp'), may hold values from -0.3125 to 0.3125
- w_value: bfloat16 [320, 1280], P(None, 'mp'), may hold values from -0.3125 to 0.3125
- w_down: bfloat16 [1280, 320], P('mp'), may hold values from -0.15625 to 0.15625
- w_out: float32 [320, 4], replicated, may hold values from -0.3125 to 0.3125
Outputs:
- next_window: float32 [4, 8, 4, 4096], P(None, 'tm')
- eps: float32 [4, 8, 4, 4096], P(None, 'tm', None, 'mp')
Inputs may be any that keep to these rules, and one draw needn't show every extreme that they name: `slide`: some prompt slides by exactly 8, and another by exactly 1.
All inputs are finite; a program needn't handle non-finite values.
Results may differ from a plain program's by a relative error of at most 0.0023.
Values sent between devices are 32-bit elements; how exact they have to be, the bound alone decides.
No kernel may reach another device: no remote copies, remote signals or barrier semaphores. Data moves between devices by JAX's collectives and lax.ppermute only.
A program may use at most 64 MiB of HBM per device.

v0:
```python
import math
import jax
import jax.numpy as jnp
from jax import lax
from jax.sharding import PartitionSpec as P

TSTEPS = 1000


def prefix(x, axis, combine, identity):
    peers, mine = (lax.axis_size(axis), lax.axis_index(axis))
    everything = lax.all_gather(x, axis)
    start = jnp.broadcast_to(jnp.asarray(identity, x.dtype), x.shape)

    def lap(k, before):
        reached = k < mine
        new = combine(before, everything[k])
        return jnp.where(reached, new, before)

    return lax.fori_loop(0, peers, lap, start)


def from_root(block, axis, holder):
    block = jnp.where(lax.axis_index(axis) == holder, block, jnp.zeros_like(block))
    return lax.psum(block, axis)


def from_behind(block, axis, distance):
    devices = range(lax.axis_size(axis))
    route = [(i - distance, i) for i in devices if i - distance in devices]
    return lax.ppermute(block, axis, route)


def plan(count):
    steps_f = jnp.arange(count, dtype=jnp.float32)
    beta = 0.0001 + (0.02 - 0.0001) * steps_f / (count - 1)
    abar = jnp.cumprod(1.0 - beta)
    return (beta, abar)


def lookup(table, times):
    grid = jnp.arange(table.shape[0], dtype=jnp.int32)
    return jnp.sum(jnp.where(times[..., None] == grid, table, 0.0), axis=-1)


def embed(times, channels):
    half = channels // 2
    freq = jnp.exp(-math.log(10000.0) * jnp.arange(half, dtype=jnp.float32) / half)
    angle = times[..., None] * freq
    return jnp.concatenate([jnp.cos(angle), jnp.sin(angle)], axis=-1)


def add_terms(earlier, later):
    return earlier + later


def shards(latents, noise, start_step, slide, w_in, w_gate, w_value, w_down, w_out):
    prompts, t_dev, lat, pos = latents.shape
    channels = w_in.shape[1]
    n_tm = lax.axis_size("tm")
    window = n_tm * t_dev
    share_width = pos // lax.axis_size("mp")
    share_offset = lax.axis_index("mp") * share_width
    slots = lax.axis_index("tm") * t_dev + jnp.arange(t_dev, dtype=jnp.int32)
    times = start_step[:, None] - slots[None, :]
    beta, abar = plan(TSTEPS)
    beta_t = lookup(beta, times)[:, :, None, None]
    abar_t = lookup(abar, times)[:, :, None, None]
    vectors = embed(times.astype(jnp.float32), channels).reshape(prompts * t_dev, channels)
    folded = jnp.dot(w_down.astype(jnp.float32), w_out, precision=lax.Precision.HIGHEST)
    items = latents.reshape(prompts * t_dev, lat, pos)

    def denoise(pair):
        latent, vector = pair
        hid = jnp.dot(w_in.T, latent, precision=lax.Precision.HIGHEST) + vector[:, None]
        mean = jnp.mean(hid, axis=0)
        var = jnp.mean((hid - mean) ** 2, axis=0)
        normed = ((hid - mean) * lax.rsqrt(var + 1e-05)).astype(jnp.bfloat16)
        gate = jnp.einsum("cf,cp->fp", w_gate, normed, preferred_element_type=jnp.float32)
        value = jnp.einsum("cf,cp->fp", w_value, normed, preferred_element_type=jnp.float32)
        hidden = (jax.nn.gelu(gate, approximate=False) * value).astype(jnp.bfloat16)
        partial_eps = jnp.dot(folded.T, hidden, precision=lax.Precision.HIGHEST)
        base_eps = jnp.dot(w_out.T, hid, precision=lax.Precision.HIGHEST)
        return (partial_eps, base_eps)

    partials, bases = lax.map(denoise, (items, vectors))
    eps = lax.psum(partials, "mp") + bases
    eps = eps.reshape(prompts, t_dev, lat, pos)
    eps_share = lax.dynamic_slice_in_dim(eps, share_offset, share_width, 3)
    stepped = (latents - beta_t / jnp.sqrt(1.0 - abar_t) * eps) / jnp.sqrt(1.0 - beta_t) + jnp.sqrt(
        beta_t
    ) * noise
    drift = stepped - latents
    first = (slots == 0)[None, :, None, None]
    head_part = jnp.where(first, latents, 0.0)
    terms = drift + head_part
    totals = jnp.sum(terms, axis=1)
    before = prefix(totals, "tm", add_terms, jnp.zeros_like(totals))
    updated = before[:, None] + (jnp.cumsum(terms, axis=1) - terms) + head_part
    last = from_root(updated[:, -1], "tm", n_tm - 1)
    moved = updated
    for bit in range((window // 2).bit_length()):
        step = 1 << bit
        incoming = from_behind(moved, "tm", -max(1, step // t_dev))
        taken = slide >> bit & 1 == 1
        moved = jnp.where(taken[:, None, None, None], incoming, moved)
    beyond = slots[None, :] + slide[:, None] >= window
    result = jnp.where(beyond[:, :, None, None], last[:, None], moved)
    return (result, eps_share)


def solution(mesh):
    in_specs = (
        P(None, "tm", None, None),
        P(None, "tm", None, None),
        P(),
        P(),
        P(),
        P(None, "mp"),
        P(None, "mp"),
        P("mp", None),
        P(),
    )
    out_specs = (P(None, "tm", None, None), P(None, "tm", None, "mp"))
    return jax.shard_map(shards, mesh=mesh, in_specs=in_specs, out_specs=out_specs, check_vma=False)
```

profile of v0, /device:TPU:0, one launch (start us, length us, event | category | flops | bytes accessed | tf_op | source)
XLA Modules:
  0.0 305.6 jit_solution(13553774158699933047)
XLA Ops:
  7.2 0.0 all-reduce.4.cloned.1.call-start
  7.3 1.2 fusion.29
  8.4 0.1 multiply_cosine_fusion
  8.6 0.1 maximum_bitcast_fusion
  8.6 1.0 fusion.31
  9.6 99.3 %while.26 = (s32[]{:T(128)}, f32[4,4,4096]{2,1,0:T(4,128)S(1)}, f32[4,4,4096]{2,1,0:T(4,128)S(1)}, f32[4,4,4096]{2,1,0:T(4,128)}, f32[4,320]{1,0:T(4,128)}, /*in...) while((s32[]{:T(128)}, f32[4,4,4096]{2,1,0:T(4,128)S(1)}, ...), condition=%wide.region_7.8_spmd, body=%wide.region_4.7_spmd.sunk | while | flops 1967394816 | bytes 44411340 | solution.py:86
  9.7 5.4 %fusion.60 = (f32[4096]{0:T(1024)S(1)}, f32[4096,320]{0,1:T(8,128)S(1)}) fusion(f32[320]{0:T(512)S(1)} %dynamic-slice_reduce_fusion.2, f32[4,320]{1,0:T(4,128)} %get-tuple-element.315, f32[4,4,4096]{2,1,0:T(4,128)} %get-tuple-element.314, s32[]{:T(128)} %get-tuple-element.300), kind=kOutput, calls=%fused_computation.72.clone.1 | convolution fusion | flops 65531904 | bytes 5332736 | tf_op jit(solution)/shard_map/while/body/eval_jaxpr/dot_general | solution.py:75
  15.1 0.6 multiply_reduce_fusion.2
  15.7 1.6 fusion.61
  17.3 13.1 %fusion.62 = bf16[320,4096]{1,0:T(8,128)(2,1)S(1)} fusion(bf16[320,320]{1,0:T(8,128)(2,1)S(1)} %copy-done.8, f32[4096,320]{0,1:T(8,128)S(1)} %fusion.61, f32[4096,320]{0,1:T(8,128)S(1)} %get-tuple-element.283, f32[4096]{0:T(1024)S(1)} %add_rsqrt_fusion.2, f32[4096]{0:T(1024)S(1)} %broadcast_multiply_fusion.2), kind=kOutput, calls=%fused_computation.5.clone.1 | convolution fusion | flops 929300480 | bytes 13344768 | tf_op jit(solution)/shard_map/while/body/eval_jaxpr/cf,cp->fp/dot_general | solution.py:80
  30.5 1.1 fusion.63
  31.6 2.8 fusion.64
  34.5 5.3 %fusion.60 = (f32[4096]{0:T(1024)S(1)}, f32[4096,320]{0,1:T(8,128)S(1)}) fusion(f32[320]{0:T(512)S(1)} %dynamic-slice_reduce_fusion.2, f32[4,320]{1,0:T(4,128)} %get-tuple-element.315, f32[4,4,4096]{2,1,0:T(4,128)} %get-tuple-element.314, s32[]{:T(128)} %get-tuple-element.300), kind=kOutput, calls=%fused_computation.72.clone.1 | convolution fusion | flops 65531904 | bytes 5332736 | tf_op jit(solution)/shard_map/while/body/eval_jaxpr/dot_general | solution.py:75
  39.9 0.6 multiply_reduce_fusion.2
  40.5 1.6 fusion.61
  42.2 13.1 %fusion.62 = bf16[320,4096]{1,0:T(8,128)(2,1)S(1)} fusion(bf16[320,320]{1,0:T(8,128)(2,1)S(1)} %copy-done.8, f32[4096,320]{0,1:T(8,128)S(1)} %fusion.61, f32[4096,320]{0,1:T(8,128)S(1)} %get-tuple-element.283, f32[4096]{0:T(1024)S(1)} %add_rsqrt_fusion.2, f32[4096]{0:T(1024)S(1)} %broadcast_multiply_fusion.2), kind=kOutput, calls=%fused_computation.5.clone.1 | convolution fusion | flops 929300480 | bytes 13344768 | tf_op jit(solution)/shard_map/while/body/eval_jaxpr/cf,cp->fp/dot_general | solution.py:80
  55.3 1.1 fusion.63
  56.5 2.8 fusion.64
  59.3 5.3 %fusion.60 = (f32[4096]{0:T(1024)S(1)}, f32[4096,320]{0,1:T(8,128)S(1)}) fusion(f32[320]{0:T(512)S(1)} %dynamic-slice_reduce_fusion.2, f32[4,320]{1,0:T(4,128)} %get-tuple-element.315, f32[4,4,4096]{2,1,0:T(4,128)} %get-tuple-element.314, s32[]{:T(128)} %get-tuple-element.300), kind=kOutput, calls=%fused_computation.72.clone.1 | convolution fusion | flops 65531904 | bytes 5332736 | tf_op jit(solution)/shard_map/while/body/eval_jaxpr/dot_general | solution.py:75
  64.7 0.6 multiply_reduce_fusion.2
  65.3 1.6 fusion.61
  67.0 13.1 %fusion.62 = bf16[320,4096]{1,0:T(8,128)(2,1)S(1)} fusion(bf16[320,320]{1,0:T(8,128)(2,1)S(1)} %copy-done.8, f32[4096,320]{0,1:T(8,128)S(1)} %fusion.61, f32[4096,320]{0,1:T(8,128)S(1)} %get-tuple-element.283, f32[4096]{0:T(1024)S(1)} %add_rsqrt_fusion.2, f32[4096]{0:T(1024)S(1)} %broadcast_multiply_fusion.2), kind=kOutput, calls=%fused_computation.5.clone.1 | convolution fusion | flops 929300480 | bytes 13344768 | tf_op jit(solution)/shard_map/while/body/eval_jaxpr/cf,cp->fp/dot_general | solution.py:80
  80.1 1.1 fusion.63
  81.3 2.8 fusion.64
  84.1 5.3 %fusion.60 = (f32[4096]{0:T(1024)S(1)}, f32[4096,320]{0,1:T(8,128)S(1)}) fusion(f32[320]{0:T(512)S(1)} %dynamic-slice_reduce_fusion.2, f32[4,320]{1,0:T(4,128)} %get-tuple-element.315, f32[4,4,4096]{2,1,0:T(4,128)} %get-tuple-element.314, s32[]{:T(128)} %get-tuple-element.300), kind=kOutput, calls=%fused_computation.72.clone.1 | convolution fusion | flops 65531904 | bytes 5332736 | tf_op jit(solution)/shard_map/while/body/eval_jaxpr/dot_general | solution.py:75
  89.5 0.6 multiply_reduce_fusion.2
  90.1 1.6 fusion.61
  91.8 13.1 %fusion.62 = bf16[320,4096]{1,0:T(8,128)(2,1)S(1)} fusion(bf16[320,320]{1,0:T(8,128)(2,1)S(1)} %copy-done.8, f32[4096,320]{0,1:T(8,128)S(1)} %fusion.61, f32[4096,320]{0,1:T(8,128)S(1)} %get-tuple-element.283, f32[4096]{0:T(1024)S(1)} %add_rsqrt_fusion.2, f32[4096]{0:T(1024)S(1)} %broadcast_multiply_fusion.2), kind=kOutput, calls=%fused_computation.5.clone.1 | convolution fusion | flops 929300480 | bytes 13344768 | tf_op jit(solution)/shard_map/while/body/eval_jaxpr/cf,cp->fp/dot_general | solution.py:80
  104.9 1.1 fusion.63
  106.1 2.8 fusion.64
  108.9 0.7 copy-done.3
  109.6 0.0 all-reduce.4.cloned.1.call-update
  109.6 0.0 all-gather.3.cloned.1.call-start
  109.7 0.3 reduce-window.9
  110.0 0.1 slice.10
  110.1 0.1 slice_reduce_fusion
  110.2 0.1 multiply_bitcast_fusion
  110.3 0.2 select_reduce_fusion
  110.5 34.3 %all-reduce.4.cloned.1.call-done = f32[4,4,4096]{2,1,0:T(4,128)} async-done(((f32[4,4,4096]{2,1,0:T(4,128)}), f32[4,4,4096]{2,1,0:T(4,128)}) %all-reduce.4.cloned.1.call-update) | async-done | bytes 262160 | tf_op jit(solution)/shard_map/psum | solution.py:87
  144.8 1.9 fusion.26
  146.7 0.0 all-gather.3.cloned.1.call-update
  146.8 0.0 all-reduce.6.cloned.1.call-start
  146.8 49.8 %all-gather.3.cloned.1.call-done = f32[32,1,4,4096]{3,2,1,0:T(4,128)} async-done(((f32[4,1,4,4096]{3,2,1,0:T(4,128)}), f32[32,1,4,4096]{3,2,1,0:T(4,128)}) %all-gather.3.cloned.1.call-update) | async-done | bytes 2097168 | tf_op jit(solution)/shard_map/all_gather | solution.py:12
  196.6 10.1 %while.27 = (s32[]{:T(128)}, f32[4,4,4096]{2,1,0:T(4,128)S(1)}, s32[]{:T(128)}, f32[8,4,4,4096]{3,2,1,0:T(4,128)}, s32[]{:T(128)}, /*index=5*/s32[]{:T(128)}) while((s32[]{:T(128)}, f32[4,4,4096]{2,1,0:T(4,128)S(1)}, s32[]{:T(128)}, f32[8,4,4,4096]{3,2,1,0:T(4,128)}, s32[]{:T(128)}, /*index=5*/s32[]{:T(128)}) %tuple.75), condition=%wide.region_10.11_spmd.clone, body=%wide.region_9.10_spmd.clone.sunk | while | flops 196612 | bytes 786525 | solution.py:20
  196.6 1.2 add_select_fusion.2
  197.9 1.2 add_select_fusion.2
  199.1 1.2 add_select_fusion.2
  200.4 1.2 add_select_fusion.2
  201.6 1.2 add_select_fusion.2
  202.9 1.2 add_select_fusion.2
  204.2 1.2 add_select_fusion.2
  205.4 1.2 add_select_fusion.2
  206.7 1.8 broadcast_select_fusion
  208.5 1.3 collective-permute-start
  209.8 6.9 %collective-permute-done = f32[4,1,4,4096]{3,2,1,0:T(4,128)S(1)} collective-permute-done((f32[4,1,4,4096]{3,2,1,0:T(4,128)S(1)}, f32[4,1,4,4096]{3,2,1,0:T(4,128)S(1)}, u32[]{:S(2)}, u32[]{:S(2)}) %collective-permute-start) | collective-permute-done | bytes 262176 | tf_op jit(solution)/shard_map/ppermute | solution.py:31
  216.7 0.1 broadcast_select_fusion.1
  216.9 1.3 collective-permute-start.1
  218.2 0.0 all-reduce.6.cloned.1.call-update
  218.2 7.1 %collective-permute-done.1 = f32[4,1,4,4096]{3,2,1,0:T(4,128)S(1)} collective-permute-done((f32[4,1,4,4096]{3,2,1,0:T(4,128)S(1)}, f32[4,1,4,4096]{3,2,1,0:T(4,128)S(1)}, u32[]{:S(2)}, u32[]{:S(2)}) %collective-permute-start.1) | collective-permute-done | bytes 262176 | tf_op jit(solution)/shard_map/ppermute | solution.py:31
  225.3 0.1 broadcast_select_fusion.2
  225.4 1.3 collective-permute-start.2
  226.7 0.6 dynamic-slice_bitcast_fusion
  227.4 69.9 %all-reduce.6.cloned.1.call-done = f32[4,1,4,4096]{3,2,1,0:T(4,128)} async-done(((f32[4,1,4,4096]{3,2,1,0:T(4,128)}), f32[4,1,4,4096]{3,2,1,0:T(4,128)}) %all-reduce.6.cloned.1.call-update) | async-done | bytes 262160 | tf_op jit(solution)/shard_map/psum | solution.py:25
  297.2 1.8 select_select_fusion
  (58 shorter events, 0.4 us)
Async XLA Ops:
  7.2 1.5 copy-start
  7.2 137.6 %all-reduce.4.cloned.1.call-start = ((), (), s32[]{:S(2)}) async-start(), calls=%async_computation | async-start | bytes 524288 | tf_op jit(solution)/shard_map/psum | solution.py:87
  9.6 100.7 %copy-start.6 = (s32[4]{0:T(128)S(1)}, s32[4]{0:T(128)}, u32[]{:S(2)}) copy-start(s32[4]{0:T(128)} %get-tuple-element.187) | copy-start | bytes 52
  9.6 135.2 %copy-start.4 = (f32[4,1,4,4096]{3,2,1,0:T(4,128)S(1)}, f32[4,1,4,4096]{3,2,1,0:T(4,128)}, u32[]{:S(2)}) copy-start(f32[4,1,4,4096]{3,2,1,0:T(4,128)} %param.14) | copy-start | bytes 786436
  9.7 6.0 %copy-start.1 = (bf16[320,320]{1,0:T(8,128)(2,1)S(1)}, bf16[320,320]{1,0:T(8,128)(2,1)}, u32[]{:S(2)}) copy-start(bf16[320,320]{1,0:T(8,128)(2,1)} %get-tuple-element.317) | copy-start | bytes 614404 | tf_op jit(solution)/shard_map/while
  15.7 1.6 copy-start.8
  17.3 14.3 %copy-start.5 = (f32[320,4]{0,1:T(4,128)S(1)}, f32[320,4]{0,1:T(4,128)}, u32[]{:S(2)}) copy-start(f32[320,4]{0,1:T(4,128)} %get-tuple-element.320) | copy-start | bytes 15364 | tf_op jit(solution)/shard_map/while
  34.5 6.0 %copy-start.1 = (bf16[320,320]{1,0:T(8,128)(2,1)S(1)}, bf16[320,320]{1,0:T(8,128)(2,1)}, u32[]{:S(2)}) copy-start(bf16[320,320]{1,0:T(8,128)(2,1)} %get-tuple-element.317) | copy-start | bytes 614404 | tf_op jit(solution)/shard_map/while
  40.5 1.6 copy-start.8
  42.1 14.3 %copy-start.5 = (f32[320,4]{0,1:T(4,128)S(1)}, f32[320,4]{0,1:T(4,128)}, u32[]{:S(2)}) copy-start(f32[320,4]{0,1:T(4,128)} %get-tuple-element.320) | copy-start | bytes 15364 | tf_op jit(solution)/shard_map/while
  59.3 6.0 %copy-start.1 = (bf16[320,320]{1,0:T(8,128)(2,1)S(1)}, bf16[320,320]{1,0:T(8,128)(2,1)}, u32[]{:S(2)}) copy-start(bf16[320,320]{1,0:T(8,128)(2,1)} %get-tuple-element.317) | copy-start | bytes 614404 | tf_op jit(solution)/shard_map/while
  65.3 1.6 copy-start.8
  67.0 14.3 %copy-start.5 = (f32[320,4]{0,1:T(4,128)S(1)}, f32[320,4]{0,1:T(4,128)}, u32[]{:S(2)}) copy-start(f32[320,4]{0,1:T(4,128)} %get-tuple-element.320) | copy-start | bytes 15364 | tf_op jit(solution)/shard_map/while
  84.1 6.0 %copy-start.1 = (bf16[320,320]{1,0:T(8,128)(2,1)S(1)}, bf16[320,320]{1,0:T(8,128)(2,1)}, u32[]{:S(2)}) copy-start(bf16[320,320]{1,0:T(8,128)(2,1)} %get-tuple-element.317) | copy-start | bytes 614404 | tf_op jit(solution)/shard_map/while
  90.1 1.6 copy-start.8
  91.8 14.3 %copy-start.5 = (f32[320,4]{0,1:T(4,128)S(1)}, f32[320,4]{0,1:T(4,128)}, u32[]{:S(2)}) copy-start(f32[320,4]{0,1:T(4,128)} %get-tuple-element.320) | copy-start | bytes 15364 | tf_op jit(solution)/shard_map/while
  108.9 0.7 copy-start.3
  108.9 97.8 %copy-start.2 = (f32[4,4,4096]{2,1,0:T(4,128)S(1)}, f32[4,4,4096]{2,1,0:T(4,128)}, u32[]{:S(2)}) copy-start(f32[4,4,4096]{2,1,0:T(4,128)} %get-tuple-element.343) | copy-start | bytes 786436
  108.9 100.8 %copy-start.7 = (s32[4]{0:T(128)S(1)}, s32[4]{0:T(128)}, u32[]{:S(2)}) copy-start(s32[4]{0:T(128)} %param.16) | copy-start | bytes 52
  109.6 87.0 %all-gather.3.cloned.1.call-start = ((), (), s32[]{:S(2)}) async-start(), calls=%async_computation.2 | async-start | bytes 2359296 | tf_op jit(solution)/shard_map/all_gather | solution.py:12
  146.8 150.5 %all-reduce.6.cloned.1.call-start = ((), (), s32[]{:S(2)}) async-start(), calls=%async_computation.1 | async-start | bytes 524288 | tf_op jit(solution)/shard_map/psum | solution.py:25
  208.5 8.3 %collective-permute-start = (f32[4,1,4,4096]{3,2,1,0:T(4,128)S(1)}, f32[4,1,4,4096]{3,2,1,0:T(4,128)S(1)}, u32[]{:S(2)}, u32[]{:S(2)}) collective-permute-start(f32[4,1,4,4096]{3,2,1,0:T(4,128)S(1)} %get-tuple-element.183), channel_id=1, source_target_pairs={{4,0},{8,4},{12,8},{16,12},{20,16},{24,20},{28,24},{5,1},{9,5},{13... | collective-permute-start | bytes 786440 | tf_op jit(solution)/shard_map/ppermute | solution.py:31
  216.9 8.4 %collective-permute-start.1 = (f32[4,1,4,4096]{3,2,1,0:T(4,128)S(1)}, f32[4,1,4,4096]{3,2,1,0:T(4,128)S(1)}, u32[]{:S(2)}, u32[]{:S(2)}) collective-permute-start(f32[4,1,4,4096]{3,2,1,0:T(4,128)S(1)} %broadcast_select_fusion.1), channel_id=1, source_target_pairs={{8,0},{12,4},{16,8},{20,12},{24,16},{28,20},{9,1},{13,5},{17,9},{2... | collective-permute-start | bytes 786440 | tf_op jit(solution)/shard_map/ppermute | solution.py:31
  225.4 71.8 %collective-permute-start.2 = (f32[4,1,4,4096]{3,2,1,0:T(4,128)S(1)}, f32[4,1,4,4096]{3,2,1,0:T(4,128)S(1)}, u32[]{:S(2)}, u32[]{:S(2)}) collective-permute-start(f32[4,1,4,4096]{3,2,1,0:T(4,128)S(1)} %broadcast_select_fusion.2), channel_id=1, source_target_pairs={{16,0},{20,4},{24,8},{28,12},{17,1},{21,5},{25,9},{29,13},{18,2},{... | collective-permute-start | bytes 786440 | tf_op jit(solution)/shard_map/ppermute | solution.py:31
Sparse Core Ops, SparseCore 0:
  109.8 34.9 all-reduce.3
  147.5 49.0 all-gather.2
  218.3 78.8 all-reduce.5
where the time goes:
time: 306 us
  waiting for transfers between devices  168 us (55%)
  matrix products  97.2 us (32%)
  other arithmetic  20.2 us (7%)
  between operations  13.9 us (5%)
  starting transfers between devices  3.99 us (1%)
    psum x1, waiting for transfers between devices, from_root(): return lax.psum(block, axis)  69.9 us
    dot_general x4, matrix products, denoise(): jnp.einsum('cf,cp->fp', w_value, normed, preferred_element_type=jnp.float32)  52.5 us
    all_gather x1, waiting for transfers between devices, prefix(): everything = lax.all_gather(x, axis)  49.8 us
    psum x1, waiting for transfers between devices, shards(): eps = lax.psum(partials, 'mp') + bases  34.3 us
    dot_general x4, matrix products, denoise(): jnp.dot(w_in.T, latent, precision=lax.Precision.HIGHEST) + vector[:, None]  21.4 us
    ppermute x3, waiting for transfers between devices, from_behind(): return lax.ppermute(block, axis, route)  14 us
    dot_general x4, matrix products, denoise(): base_eps = jnp.dot(w_out.T, hid, precision=lax.Precision.HIGHEST)  11.3 us
    select_n x8, other arithmetic, lap(): return jnp.where(reached, new, before)  9.92 us
  transfers between devices with their start and end apart: 6, of which 5 were waited for; matrix products, arithmetic and copies ran while one was open for 1% of the time, Pallas kernels for 0%

commit v1 on v0

--- a/solution.py
+++ b/solution.py
@@ -84,7 +84,7 @@
         return (partial_eps, base_eps)
 
     partials, bases = lax.map(denoise, (items, vectors))
-    eps = lax.psum(partials, "mp") + bases
+    eps = jnp.sum(lax.all_gather(partials, axis_name="mp"), axis=0) + bases
     eps = eps.reshape(prompts, t_dev, lat, pos)
     eps_share = lax.dynamic_slice_in_dim(eps, share_offset, share_width, 3)
     stepped = (latents - beta_t / jnp.sqrt(1.0 - abar_t) * eps) / jnp.sqrt(1.0 - beta_t) + jnp.sqrt(

time: 306 us -> 292 us (0.954)
  waiting for transfers between devices: 168 us -> 152 us
    psum x1 -> x0, waiting for transfers between devices: 34.3 us -> none  [shards(): eps = lax.psum(partials, 'mp') + bases]
    all_gather x0 -> x1, waiting for transfers between devices: none -> 18.7 us  [shards(): eps = jnp.sum(lax.all_gather(partials, axis_name='mp'), axis=0) + bases]
where the time goes in v1:
time: 292 us; the launch traced here: 291 us
  waiting for transfers between devices  152 us (52%)
  matrix products  97.2 us (33%)
  other arithmetic  21.6 us (7%)
  between operations  13.9 us (5%)
  starting transfers between devices  3.99 us (1%)
    psum x1, waiting for transfers between devices, from_root(): return lax.psum(block, axis)  69.9 us
    dot_general x4, matrix products, denoise(): jnp.einsum('cf,cp->fp', w_value, normed, preferred_element_type=jnp.float32)  52.5 us
    all_gather x1, waiting for transfers between devices, prefix(): everything = lax.all_gather(x, axis)  49.2 us
    dot_general x4, matrix products, denoise(): jnp.dot(w_in.T, latent, precision=lax.Precision.HIGHEST) + vector[:, None]  21.4 us
    all_gather x1, waiting for transfers between devices, shards(): eps = jnp.sum(lax.all_gather(partials, axis_name='mp'), axis=0) + bases  18.7 us
    ppermute x3, waiting for transfers between devices, from_behind(): return lax.ppermute(block, axis, route)  14 us
    dot_general x4, matrix products, denoise(): base_eps = jnp.dot(w_out.T, hid, precision=lax.Precision.HIGHEST)  11.3 us
    select_n x8, other arithmetic, lap(): return jnp.where(reached, new, before)  9.92 us
  transfers between devices with their start and end apart: 6, of which 5 were waited for; matrix products, arithmetic and copies ran while one was open for 1% of the time, Pallas kernels for 0%

profile of v1, /device:TPU:0, one launch (start us, length us, event | category | flops | bytes accessed | tf_op | source)
XLA Modules:
  0.0 290.9 jit_solution(6478198163352663730)
XLA Ops:
  7.2 0.0 all-gather.5.cloned.1.call-start
  7.3 1.2 fusion.29
  8.5 0.1 multiply_cosine_fusion
  8.6 0.1 maximum_bitcast_fusion
  8.7 1.0 fusion.31
  9.7 99.3 %while.26 = (s32[]{:T(128)}, f32[4,4,4096]{2,1,0:T(4,128)S(1)}, f32[4,4,4096]{2,1,0:T(4,128)S(1)}, f32[4,4,4096]{2,1,0:T(4,128)}, f32[4,320]{1,0:T(4,128)}, /*in...) while((s32[]{:T(128)}, f32[4,4,4096]{2,1,0:T(4,128)S(1)}, ...), condition=%wide.region_7.8_spmd, body=%wide.region_4.7_spmd.sunk | while | flops 1967394816 | bytes 44411340 | solution.py:86
  9.7 5.4 %fusion.60 = (f32[4096]{0:T(1024)S(1)}, f32[4096,320]{0,1:T(8,128)S(1)}) fusion(f32[320]{0:T(512)S(1)} %dynamic-slice_reduce_fusion.2, f32[4,320]{1,0:T(4,128)} %get-tuple-element.315, f32[4,4,4096]{2,1,0:T(4,128)} %get-tuple-element.314, s32[]{:T(128)} %get-tuple-element.300), kind=kOutput, calls=%fused_computation.72.clone.1 | convolution fusion | flops 65531904 | bytes 5332736 | tf_op jit(solution)/shard_map/while/body/eval_jaxpr/dot_general | solution.py:75
  15.1 0.6 multiply_reduce_fusion.2
  15.8 1.6 fusion.61
  17.4 13.1 %fusion.62 = bf16[320,4096]{1,0:T(8,128)(2,1)S(1)} fusion(bf16[320,320]{1,0:T(8,128)(2,1)S(1)} %copy-done.8, f32[4096,320]{0,1:T(8,128)S(1)} %fusion.61, f32[4096,320]{0,1:T(8,128)S(1)} %get-tuple-element.283, f32[4096]{0:T(1024)S(1)} %add_rsqrt_fusion.2, f32[4096]{0:T(1024)S(1)} %broadcast_multiply_fusion.2), kind=kOutput, calls=%fused_computation.5.clone.1 | convolution fusion | flops 929300480 | bytes 13344768 | tf_op jit(solution)/shard_map/while/body/eval_jaxpr/cf,cp->fp/dot_general | solution.py:80
  30.5 1.1 fusion.63
  31.7 2.8 fusion.64
  34.6 5.3 %fusion.60 = (f32[4096]{0:T(1024)S(1)}, f32[4096,320]{0,1:T(8,128)S(1)}) fusion(f32[320]{0:T(512)S(1)} %dynamic-slice_reduce_fusion.2, f32[4,320]{1,0:T(4,128)} %get-tuple-element.315, f32[4,4,4096]{2,1,0:T(4,128)} %get-tuple-element.314, s32[]{:T(128)} %get-tuple-element.300), kind=kOutput, calls=%fused_computation.72.clone.1 | convolution fusion | flops 65531904 | bytes 5332736 | tf_op jit(solution)/shard_map/while/body/eval_jaxpr/dot_general | solution.py:75
  39.9 0.6 multiply_reduce_fusion.2
  40.6 1.6 fusion.61
  42.2 13.1 %fusion.62 = bf16[320,4096]{1,0:T(8,128)(2,1)S(1)} fusion(bf16[320,320]{1,0:T(8,128)(2,1)S(1)} %copy-done.8, f32[4096,320]{0,1:T(8,128)S(1)} %fusion.61, f32[4096,320]{0,1:T(8,128)S(1)} %get-tuple-element.283, f32[4096]{0:T(1024)S(1)} %add_rsqrt_fusion.2, f32[4096]{0:T(1024)S(1)} %broadcast_multiply_fusion.2), kind=kOutput, calls=%fused_computation.5.clone.1 | convolution fusion | flops 929300480 | bytes 13344768 | tf_op jit(solution)/shard_map/while/body/eval_jaxpr/cf,cp->fp/dot_general | solution.py:80
  55.3 1.1 fusion.63
  56.5 2.8 fusion.64
  59.4 5.3 %fusion.60 = (f32[4096]{0:T(1024)S(1)}, f32[4096,320]{0,1:T(8,128)S(1)}) fusion(f32[320]{0:T(512)S(1)} %dynamic-slice_reduce_fusion.2, f32[4,320]{1,0:T(4,128)} %get-tuple-element.315, f32[4,4,4096]{2,1,0:T(4,128)} %get-tuple-element.314, s32[]{:T(128)} %get-tuple-element.300), kind=kOutput, calls=%fused_computation.72.clone.1 | convolution fusion | flops 65531904 | bytes 5332736 | tf_op jit(solution)/shard_map/while/body/eval_jaxpr/dot_general | solution.py:75
  64.7 0.6 multiply_reduce_fusion.2
  65.4 1.6 fusion.61
  67.0 13.1 %fusion.62 = bf16[320,4096]{1,0:T(8,128)(2,1)S(1)} fusion(bf16[320,320]{1,0:T(8,128)(2,1)S(1)} %copy-done.8, f32[4096,320]{0,1:T(8,128)S(1)} %fusion.61, f32[4096,320]{0,1:T(8,128)S(1)} %get-tuple-element.283, f32[4096]{0:T(1024)S(1)} %add_rsqrt_fusion.2, f32[4096]{0:T(1024)S(1)} %broadcast_multiply_fusion.2), kind=kOutput, calls=%fused_computation.5.clone.1 | convolution fusion | flops 929300480 | bytes 13344768 | tf_op jit(solution)/shard_map/while/body/eval_jaxpr/cf,cp->fp/dot_general | solution.py:80
  80.1 1.1 fusion.63
  81.3 2.8 fusion.64
  84.2 5.3 %fusion.60 = (f32[4096]{0:T(1024)S(1)}, f32[4096,320]{0,1:T(8,128)S(1)}) fusion(f32[320]{0:T(512)S(1)} %dynamic-slice_reduce_fusion.2, f32[4,320]{1,0:T(4,128)} %get-tuple-element.315, f32[4,4,4096]{2,1,0:T(4,128)} %get-tuple-element.314, s32[]{:T(128)} %get-tuple-element.300), kind=kOutput, calls=%fused_computation.72.clone.1 | convolution fusion | flops 65531904 | bytes 5332736 | tf_op jit(solution)/shard_map/while/body/eval_jaxpr/dot_general | solution.py:75
  89.5 0.6 multiply_reduce_fusion.2
  90.2 1.6 fusion.61
  91.8 13.1 %fusion.62 = bf16[320,4096]{1,0:T(8,128)(2,1)S(1)} fusion(bf16[320,320]{1,0:T(8,128)(2,1)S(1)} %copy-done.8, f32[4096,320]{0,1:T(8,128)S(1)} %fusion.61, f32[4096,320]{0,1:T(8,128)S(1)} %get-tuple-element.283, f32[4096]{0:T(1024)S(1)} %add_rsqrt_fusion.2, f32[4096]{0:T(1024)S(1)} %broadcast_multiply_fusion.2), kind=kOutput, calls=%fused_computation.5.clone.1 | convolution fusion | flops 929300480 | bytes 13344768 | tf_op jit(solution)/shard_map/while/body/eval_jaxpr/cf,cp->fp/dot_general | solution.py:80
  105.0 1.1 fusion.63
  106.1 2.8 fusion.64
  109.0 0.7 copy-done.3
  109.6 0.0 all-gather.5.cloned.1.call-update
  109.7 0.0 all-gather.7.cloned.1.call-start
  109.8 0.3 reduce-window.9
  110.0 0.1 slice.10
  110.1 0.1 slice_reduce_fusion
  110.3 0.1 multiply_bitcast_fusion
  110.3 0.2 select_reduce_fusion
  110.5 18.7 %all-gather.5.cloned.1.call-done = f32[16,4,4096]{2,1,0:T(4,128)} async-done(((f32[4,4,4096]{2,1,0:T(4,128)}), f32[16,4,4096]{2,1,0:T(4,128)}) %all-gather.5.cloned.1.call-update) | async-done | bytes 1048592 | tf_op jit(solution)/shard_map/all_gather | solution.py:87
  129.3 1.5 reduce_sum.51
  130.8 1.9 fusion.26
  132.7 0.0 all-reduce.3.cloned.1.call-start
  132.7 49.2 %all-gather.7.cloned.1.call-done = f32[32,1,4,4096]{3,2,1,0:T(4,128)} async-done(((f32[4,1,4,4096]{3,2,1,0:T(4,128)}), f32[32,1,4,4096]{3,2,1,0:T(4,128)}) %all-gather.7.cloned.1.call-update) | async-done | bytes 2097168 | tf_op jit(solution)/shard_map/all_gather | solution.py:12
  181.9 10.1 %while.27 = (s32[]{:T(128)}, f32[4,4,4096]{2,1,0:T(4,128)S(1)}, s32[]{:T(128)}, f32[8,4,4,4096]{3,2,1,0:T(4,128)}, s32[]{:T(128)}, /*index=5*/s32[]{:T(128)}) while((s32[]{:T(128)}, f32[4,4,4096]{2,1,0:T(4,128)S(1)}, s32[]{:T(128)}, f32[8,4,4,4096]{3,2,1,0:T(4,128)}, s32[]{:T(128)}, /*index=5*/s32[]{:T(128)}) %tuple.75), condition=%wide.region_10.11_spmd.clone, body=%wide.region_9.10_spmd.clone.sunk | while | flops 196612 | bytes 786525 | solution.py:20
  181.9 1.2 add_select_fusion.2
  183.2 1.2 add_select_fusion.2
  184.4 1.2 add_select_fusion.2
  185.7 1.2 add_select_fusion.2
  186.9 1.2 add_select_fusion.2
  188.2 1.2 add_select_fusion.2
  189.5 1.2 add_select_fusion.2
  190.7 1.2 add_select_fusion.2
  192.0 1.8 broadcast_select_fusion
  193.8 1.3 collective-permute-start
  195.1 6.9 %collective-permute-done = f32[4,1,4,4096]{3,2,1,0:T(4,128)S(1)} collective-permute-done((f32[4,1,4,4096]{3,2,1,0:T(4,128)S(1)}, f32[4,1,4,4096]{3,2,1,0:T(4,128)S(1)}, u32[]{:S(2)}, u32[]{:S(2)}) %collective-permute-start) | collective-permute-done | bytes 262176 | tf_op jit(solution)/shard_map/ppermute | solution.py:31
  202.0 0.1 broadcast_select_fusion.1
  202.2 1.3 collective-permute-start.1
  203.5 0.0 all-reduce.3.cloned.1.call-update
  203.5 7.1 %collective-permute-done.1 = f32[4,1,4,4096]{3,2,1,0:T(4,128)S(1)} collective-permute-done((f32[4,1,4,4096]{3,2,1,0:T(4,128)S(1)}, f32[4,1,4,4096]{3,2,1,0:T(4,128)S(1)}, u32[]{:S(2)}, u32[]{:S(2)}) %collective-permute-start.1) | collective-permute-done | bytes 262176 | tf_op jit(solution)/shard_map/ppermute | solution.py:31
  210.6 0.1 broadcast_select_fusion.2
  210.7 1.3 collective-permute-start.2
  212.0 0.6 dynamic-slice_bitcast_fusion
  212.7 69.9 %all-reduce.3.cloned.1.call-done = f32[4,1,4,4096]{3,2,1,0:T(4,128)} async-done(((f32[4,1,4,4096]{3,2,1,0:T(4,128)}), f32[4,1,4,4096]{3,2,1,0:T(4,128)}) %all-reduce.3.cloned.1.call-update) | async-done | bytes 262160 | tf_op jit(solution)/shard_map/psum | solution.py:25
  282.5 1.8 select_select_fusion
  (59 shorter events, 0.4 us)
Async XLA Ops:
  7.2 1.5 copy-start
  7.2 122.1 %all-gather.5.cloned.1.call-start = ((), (), s32[]{:S(2)}) async-start(), calls=%async_computation.1 | async-start | bytes 1310720 | tf_op jit(solution)/shard_map/all_gather | solution.py:87
  9.6 100.7 %copy-start.6 = (s32[4]{0:T(128)S(1)}, s32[4]{0:T(128)}, u32[]{:S(2)}) copy-start(s32[4]{0:T(128)} %get-tuple-element.187) | copy-start | bytes 52
  9.7 121.1 %copy-start.4 = (f32[4,1,4,4096]{3,2,1,0:T(4,128)S(1)}, f32[4,1,4,4096]{3,2,1,0:T(4,128)}, u32[]{:S(2)}) copy-start(f32[4,1,4,4096]{3,2,1,0:T(4,128)} %param.14) | copy-start | bytes 786436
  9.7 6.0 %copy-start.1 = (bf16[320,320]{1,0:T(8,128)(2,1)S(1)}, bf16[320,320]{1,0:T(8,128)(2,1)}, u32[]{:S(2)}) copy-start(bf16[320,320]{1,0:T(8,128)(2,1)} %get-tuple-element.317) | copy-start | bytes 614404 | tf_op jit(solution)/shard_map/while
  15.8 1.6 copy-start.8
  17.4 14.3 %copy-start.5 = (f32[320,4]{0,1:T(4,128)S(1)}, f32[320,4]{0,1:T(4,128)}, u32[]{:S(2)}) copy-start(f32[320,4]{0,1:T(4,128)} %get-tuple-element.320) | copy-start | bytes 15364 | tf_op jit(solution)/shard_map/while
  34.6 6.0 %copy-start.1 = (bf16[320,320]{1,0:T(8,128)(2,1)S(1)}, bf16[320,320]{1,0:T(8,128)(2,1)}, u32[]{:S(2)}) copy-start(bf16[320,320]{1,0:T(8,128)(2,1)} %get-tuple-element.317) | copy-start | bytes 614404 | tf_op jit(solution)/shard_map/while
  40.6 1.6 copy-start.8
  42.2 14.3 %copy-start.5 = (f32[320,4]{0,1:T(4,128)S(1)}, f32[320,4]{0,1:T(4,128)}, u32[]{:S(2)}) copy-start(f32[320,4]{0,1:T(4,128)} %get-tuple-element.320) | copy-start | bytes 15364 | tf_op jit(solution)/shard_map/while
  59.3 6.0 %copy-start.1 = (bf16[320,320]{1,0:T(8,128)(2,1)S(1)}, bf16[320,320]{1,0:T(8,128)(2,1)}, u32[]{:S(2)}) copy-start(bf16[320,320]{1,0:T(8,128)(2,1)} %get-tuple-element.317) | copy-start | bytes 614404 | tf_op jit(solution)/shard_map/while
  65.4 1.6 copy-start.8
  67.0 14.3 %copy-start.5 = (f32[320,4]{0,1:T(4,128)S(1)}, f32[320,4]{0,1:T(4,128)}, u32[]{:S(2)}) copy-start(f32[320,4]{0,1:T(4,128)} %get-tuple-element.320) | copy-start | bytes 15364 | tf_op jit(solution)/shard_map/while
  84.2 6.0 %copy-start.1 = (bf16[320,320]{1,0:T(8,128)(2,1)S(1)}, bf16[320,320]{1,0:T(8,128)(2,1)}, u32[]{:S(2)}) copy-start(bf16[320,320]{1,0:T(8,128)(2,1)} %get-tuple-element.317) | copy-start | bytes 614404 | tf_op jit(solution)/shard_map/while
  90.2 1.6 copy-start.8
  91.8 14.3 %copy-start.5 = (f32[320,4]{0,1:T(4,128)S(1)}, f32[320,4]{0,1:T(4,128)}, u32[]{:S(2)}) copy-start(f32[320,4]{0,1:T(4,128)} %get-tuple-element.320) | copy-start | bytes 15364 | tf_op jit(solution)/shard_map/while
  108.9 0.7 copy-start.3
  109.0 83.0 %copy-start.2 = (f32[4,4,4096]{2,1,0:T(4,128)S(1)}, f32[4,4,4096]{2,1,0:T(4,128)}, u32[]{:S(2)}) copy-start(f32[4,4,4096]{2,1,0:T(4,128)} %get-tuple-element.343) | copy-start | bytes 786436
  109.0 86.1 %copy-start.7 = (s32[4]{0:T(128)S(1)}, s32[4]{0:T(128)}, u32[]{:S(2)}) copy-start(s32[4]{0:T(128)} %param.16) | copy-start | bytes 52
  109.7 72.2 %all-gather.7.cloned.1.call-start = ((), (), s32[]{:S(2)}) async-start(), calls=%async_computation.2 | async-start | bytes 2359296 | tf_op jit(solution)/shard_map/all_gather | solution.py:12
  132.7 149.9 %all-reduce.3.cloned.1.call-start = ((), (), s32[]{:S(2)}) async-start(), calls=%async_computation | async-start | bytes 524288 | tf_op jit(solution)/shard_map/psum | solution.py:25
  193.8 8.3 %collective-permute-start = (f32[4,1,4,4096]{3,2,1,0:T(4,128)S(1)}, f32[4,1,4,4096]{3,2,1,0:T(4,128)S(1)}, u32[]{:S(2)}, u32[]{:S(2)}) collective-permute-start(f32[4,1,4,4096]{3,2,1,0:T(4,128)S(1)} %get-tuple-element.183), channel_id=1, source_target_pairs={{4,0},{8,4},{12,8},{16,12},{20,16},{24,20},{28,24},{5,1},{9,5},{13... | collective-permute-start | bytes 786440 | tf_op jit(solution)/shard_map/ppermute | solution.py:31
  202.2 8.4 %collective-permute-start.1 = (f32[4,1,4,4096]{3,2,1,0:T(4,128)S(1)}, f32[4,1,4,4096]{3,2,1,0:T(4,128)S(1)}, u32[]{:S(2)}, u32[]{:S(2)}) collective-permute-start(f32[4,1,4,4096]{3,2,1,0:T(4,128)S(1)} %broadcast_select_fusion.1), channel_id=1, source_target_pairs={{8,0},{12,4},{16,8},{20,12},{24,16},{28,20},{9,1},{13,5},{17,9},{2... | collective-permute-start | bytes 786440 | tf_op jit(solution)/shard_map/ppermute | solution.py:31
  210.7 71.8 %collective-permute-start.2 = (f32[4,1,4,4096]{3,2,1,0:T(4,128)S(1)}, f32[4,1,4,4096]{3,2,1,0:T(4,128)S(1)}, u32[]{:S(2)}, u32[]{:S(2)}) collective-permute-start(f32[4,1,4,4096]{3,2,1,0:T(4,128)S(1)} %broadcast_select_fusion.2), channel_id=1, source_target_pairs={{16,0},{20,4},{24,8},{28,12},{17,1},{21,5},{25,9},{29,13},{18,2},{... | collective-permute-start | bytes 786440 | tf_op jit(solution)/shard_map/ppermute | solution.py:31
Sparse Core Ops, SparseCore 0:
  109.8 19.4 all-gather.4
  132.8 49.0 all-gather.6
  203.6 78.8 all-reduce.2
